TPU v7x, 32 devices: a 4x2x2 block of a 4x4x8 slice. The times are simulated.
32 devices in a mesh: dp: 4 (over y, z), ctx: 8 (over x, core).
Axes of the slice: x: 4, y: 2, z: 2, core: 2. Of those that a mesh axis runs over, the one named last changes fastest.
The devices are a block of a 4x4x8 slice.
Arguments:
- hidden: bfloat16 [1024, 2048], P(('dp', 'ctx')), parts along dimension 0
- w_q: bfloat16 [2048, 3072], replicated
- w_uk: bfloat16 [16, 128, 512], replicated
- w_uv: bfloat16 [16, 512, 128], replicated
- w_o: bfloat16 [2048, 2048], replicated
- kv_prefix: bfloat16 [65536, 576], P(('dp', 'ctx')), parts along dimension 0
- kv_suffix: bfloat16 [1024, 1024, 576], P(('dp', 'ctx')), parts along dimension 0
- seq_lens: int32 [1024], P(('dp', 'ctx')), parts along dimension 0
Outputs:
- output: bfloat16 [1024, 2048], P(('dp', 'ctx')), parts along dimension 0
There are 4 independent parts. A program takes and returns all parts, laid end to end along the dimension named above; an argument that names none is the same for every part.
All inputs are finite; a program needn't handle non-finite values.
Results may differ from a plain program's by a relative error of at most 0.00660993.
Values are sent between devices in bfloat16 or wider.
A program may use at most 768 MiB of HBM per device.

v0:
```python
import math
import jax
import jax.numpy as jnp
from jax import lax
from jax.sharding import PartitionSpec as P

ROPE_BASE = 10000


def rope_rotate(rot_in, positions):
    half_dim = rot_in.shape[-1] // 2
    inv_freq = jnp.exp(jnp.arange(half_dim, dtype=jnp.float32) * (-math.log(ROPE_BASE) / half_dim))
    angle = positions.astype(jnp.float32)[:, None, None] * inv_freq
    cos_part = jnp.cos(angle)
    sin_part = jnp.sin(angle)
    rot_wide = rot_in.astype(jnp.float32)
    first_half = rot_wide[..., :half_dim]
    second_half = rot_wide[..., half_dim:]
    return jnp.concatenate([first_half * cos_part - second_half * sin_part, second_half * cos_part + first_half * sin_part], axis=-1)


def make_query(hidden, w_q, w_uk, positions):
    rows = hidden.shape[0]
    heads, nope_dim = w_uk.shape[0], w_uk.shape[1]
    q_all = jnp.dot(hidden, w_q, preferred_element_type=jnp.float32).astype(jnp.bfloat16).reshape(rows, heads, -1)
    q_lat = jnp.einsum('bhn,hnc->bhc', q_all[..., :nope_dim], w_uk, preferred_element_type=jnp.float32).astype(jnp.bfloat16)
    q_rot = rope_rotate(q_all[..., nope_dim:], positions).astype(jnp.bfloat16)
    return jnp.concatenate([q_lat, q_rot], axis=-1)


def suffix_scores(query, kv_suffix, seq_lens, scale):
    s_suf = jnp.einsum('bhw,bsw->bhs', query, kv_suffix, preferred_element_type=jnp.float32) * scale
    slots = jnp.arange(kv_suffix.shape[1])
    return jnp.where(slots[None, None, :] <= seq_lens[:, None, None], s_suf, -jnp.inf)


def finish_output(hidden, o_lat, w_uv, w_o):
    o_val = jnp.einsum('bhc,hcv->bhv', o_lat, w_uv, preferred_element_type=jnp.float32).astype(jnp.bfloat16)
    out_proj = jnp.dot(o_val.reshape(hidden.shape[0], -1), w_o, preferred_element_type=jnp.float32)
    return (hidden.astype(jnp.float32) + out_proj).astype(jnp.bfloat16)


def solution(mesh):
    group = mesh.shape['ctx']
    rows_spec = P(('dp', 'ctx'), None)
    whole_spec = P()

    def local_step(hidden, w_q, w_uk, w_uv, w_o, kv_prefix, kv_suffix, seq_lens):
        rows = hidden.shape[0]
        lat_dim = w_uk.shape[2]
        prefix_len = kv_prefix.shape[0] * group
        scale = (w_q.shape[1] // w_uk.shape[0]) ** -0.5
        query = make_query(hidden, w_q, w_uk, prefix_len + seq_lens)
        q_group = lax.all_gather(query, 'ctx', axis=0, tiled=True)
        s_pre = jnp.einsum('bhw,pw->bhp', q_group, kv_prefix, preferred_element_type=jnp.float32) * scale
        m_pre = lax.pmax(jnp.max(s_pre, axis=-1), 'ctx')
        e_pre = jnp.exp(s_pre - m_pre[..., None])
        l_pre = jnp.sum(e_pre, axis=-1)
        o_pre = jnp.einsum('bhp,pc->bhc', e_pre.astype(jnp.bfloat16), kv_prefix[:, :lat_dim], preferred_element_type=jnp.float32)
        o_home = lax.psum_scatter(o_pre, 'ctx', scatter_dimension=0, tiled=True)
        l_home = lax.psum_scatter(l_pre, 'ctx', scatter_dimension=0, tiled=True)
        m_home = lax.dynamic_slice_in_dim(m_pre, lax.axis_index('ctx') * rows, rows, axis=0)
        s_suf = suffix_scores(query, kv_suffix, seq_lens, scale)
        m_all = jnp.maximum(m_home, jnp.max(s_suf, axis=-1))
        pre_weight = jnp.exp(m_home - m_all)
        e_suf = jnp.exp(s_suf - m_all[..., None])
        norm_sum = l_home * pre_weight + jnp.sum(e_suf, axis=-1)
        suf_part = jnp.einsum('bhs,bsc->bhc', e_suf.astype(jnp.bfloat16), kv_suffix[..., :lat_dim], preferred_element_type=jnp.float32)
        o_lat = ((o_home * pre_weight[..., None] + suf_part) / norm_sum[..., None]).astype(jnp.bfloat16)
        return finish_output(hidden, o_lat, w_uv, w_o)

    return jax.shard_map(local_step, mesh=mesh, in_specs=(rows_spec, whole_spec, whole_spec, whole_spec, whole_spec, rows_spec, P(('dp', 'ctx'), None, None), P(('dp', 'ctx'))), out_specs=rows_spec, check_vma=False)
```

profile of v0, /device:TPU:81, one launch (start us, length us, event | category | flops | bytes accessed | tf_op | source)
XLA Modules:
  0.0 206.1 jit_solution(11832569800873536950)
XLA Ops:
  6.5 0.0 copy-start
  6.6 0.0 all-gather.2.cloned.1.call-start
  6.6 0.0 copy-start.4
  6.6 7.1 %convolution_convert_fusion = bf16[32,3072]{1,0:T(8,128)(2,1)S(1)} fusion(bf16[32,2048]{1,0:T(8,128)(2,1)} %param.8, bf16[2048,3072]{1,0:T(8,128)(2,1)} %param.9), kind=kOutput, calls=%fused_computation.9 | convolution fusion | flops 402751488 | bytes 12910592 | tf_op jit(solution)/shard_map/dot_general | solution.py:25
  13.6 0.3 reshape.90
  14.0 0.0 copy-done.4
  14.1 0.1 multiply_cosine_fusion
  14.2 0.0 copy-done
  14.2 0.4 fusion.16
  14.6 0.1 subtract_convert_fusion
  14.8 1.0 pad_maximum_fusion
  15.8 0.1 all-gather.2.cloned.1.call-update
  15.8 0.1 reduce-scatter.7.cloned.1.call-start
  15.9 37.7 %all-gather.2.cloned.1.call-done = bf16[256,16,576]{2,0,1:T(8,128)(2,1)} async-done(((bf16[32,16,576]{2,0,1:T(8,128)(2,1)}), bf16[256,16,576]{2,0,1:T(8,128)(2,1)}) %all-gather.2.cloned.1.call-update) | async-done | bytes 4718608 | tf_op jit(solution)/shard_map/all_gather | solution.py:54
  53.6 21.8 %multiply_reduce_fusion = (f32[256,16]{0,1:T(8,128)S(1)}, f32[256,16,2048]{2,0,1:T(8,128)}) fusion(bf16[256,16,576]{2,0,1:T(8,128)(2,1)} %all-gather.2.cloned.1.call-done, bf16[2048,576]{0,1:T(8,128)(2,1)} %param.13), kind=kOutput, calls=%fused_computation.3 | convolution fusion | flops 9680449536 | bytes 40648704 | tf_op jit(solution)/shard_map/bhw,pw->bhp/dot_general | solution.py:55
  75.3 20.8 %pmax.7 = f32[256,16]{0,1:T(8,128)S(1)} all-reduce(f32[256,16]{0,1:T(8,128)S(1)} %get-tuple-element.13), channel_id=1, replica_groups=mesh['dp'=4,'ctx'=8] {'ctx'}, use_global_device_ids=true, to_apply=%region_1.0 | all-reduce | flops 4096 | bytes 32768 | tf_op jit(solution)/shard_map/pmax | solution.py:56
  96.2 14.0 %fusion.2 = f32[256,16]{0,1:T(8,128)S(1)} fusion(f32[256,16,2048]{2,0,1:T(8,128)} %get-tuple-element.14, f32[256,16]{0,1:T(8,128)S(1)} %pmax.7), kind=kLoop, calls=%fused_computation.4 | loop fusion | flops 25161728 | bytes 33587200 | tf_op jit(solution)/shard_map/reduce_sum | solution.py:58
  110.2 0.8 copy.39
  111.0 0.1 reduce-scatter.7.cloned.1.call-update
  111.0 0.2 reduce-scatter.5.cloned.1.call-start
  111.3 17.7 %fusion.4 = f32[256,16,512]{2,0,1:T(8,128)} fusion(f32[256,16,2048]{2,0,1:T(8,128)} %get-tuple-element.14, f32[256,16]{0,1:T(8,128)S(1)} %pmax.7, bf16[2048,576]{0,1:T(8,128)(2,1)} %param.13), kind=kOutput, calls=%fused_computation.6 | convolution fusion | flops 8615100416 | bytes 44056576 | tf_op jit(solution)/shard_map/bhp,pc->bhc/dot_general | solution.py:59
  129.0 0.0 copy-start.2
  129.0 0.1 reduce-scatter.5.cloned.1.call-update
  129.1 0.1 iota_compare_fusion
  129.2 0.9 copy-done.2
  130.1 14.7 %fusion.13 = (f32[32,16]{1,0:T(8,128)S(1)}, f32[32,16,1024]{2,1,0:T(8,128)S(1)}) fusion(pred[32,1024]{1,0:T(8,128)(4,1)S(1)} %iota_compare_fusion, bf16[32,1024,576]{1,2,0:T(8,128)(2,1)} %param.14, bf16[32,16,576]{2,0,1:T(8,128)(2,1)S(1)} %copy-done.2), kind=kOutput, calls=%fused_computation.18 | convolution fusion | flops 605552128 | bytes 40470528 | tf_op jit(solution)/shard_map/bhw,bsw->bhs/dot_general | solution.py:32
  144.8 0.1 copy.33
  144.9 0.1 dynamic-slice_maximum_fusion
  145.0 0.1 copy.34
  145.0 0.6 fusion.14
  145.7 0.1 copy.37
  145.7 15.1 %fusion = f32[32,16,512]{2,1,0:T(8,128)} fusion(bf16[32,1024,576]{1,2,0:T(8,128)(2,1)} %param.14, f32[32,16,1024]{2,1,0:T(8,128)S(1)} %get-tuple-element.12, f32[32,16]{1,0:T(8,128)S(1)} %copy.34, pred[32,1024]{1,0:T(8,128)(4,1)S(1)} %iota_compare_fusion), kind=kOutput, calls=%fused_computation | convolution fusion | flops 538968064 | bytes 36734976 | tf_op jit(solution)/shard_map/bhs,bsc->bhc/dot_general | solution.py:68
  160.9 0.0 reduce-scatter.7.cloned.1.call-done
  160.9 0.8 copy.40
  161.7 0.1 multiply_add_fusion
  161.8 28.9 %reduce-scatter.5.cloned.1.call-done = f32[32,16,512]{2,0,1:T(8,128)} async-done(((f32[256,16,512]{2,0,1:T(8,128)}), f32[32,16,512]{2,0,1:T(8,128)}) %reduce-scatter.5.cloned.1.call-update) | async-done | bytes 1048592 | tf_op jit(solution)/shard_map/reduce_scatter | solution.py:60
  190.7 0.0 copy-start.3
  190.7 3.1 %fusion.17 = bf16[16,4,8,128]{3,2,1,0:T(8,128)(2,1)S(1)} fusion(bf16[16,512,128]{2,1,0:T(8,128)(2,1)} %param.11, f32[32,16,512]{2,1,0:T(8,128)} %fusion, f32[32,16,512]{2,0,1:T(8,128)} %reduce-scatter.5.cloned.1.call-done, f32[32,16]{0,1:T(8,128)S(1)} %get-tuple-element.5, f32[32,16]{0,1:T(8,128)S(1)} %get-tuple-element.6), kind=kOutput, calls=%fused_computation.24 | convolution fusion | flops 68222976 | bytes 4329472 | tf_op jit(solution)/shard_map/bhc,hcv->bhv/dot_general | solution.py:38
  193.8 0.0 copy-done.3
  193.8 0.0 copy-start.1
  193.8 5.8 %fusion.10 = bf16[32,2048]{1,0:T(8,128)(2,1)} fusion(bf16[2048,2048]{1,0:T(8,128)(2,1)} %param.12, bf16[32,2048]{1,0:T(8,128)(2,1)S(1)} %copy-done.3, bf16[16,4,8,128]{3,2,1,0:T(8,128)(2,1)S(1)} %fusion.17), kind=kOutput, calls=%fused_computation.13 | convolution fusion | flops 268632064 | bytes 8781824 | tf_op jit(solution)/shard_map/dot_general | solution.py:39
  199.6 0.0 copy-done.1
  (5 shorter events, 0.1 us)
Async XLA Ops:
  6.5 7.7 %copy-start = (bf16[16,128,512]{2,1,0:T(8,128)(2,1)S(1)}, bf16[16,128,512]{2,1,0:T(8,128)(2,1)}, u32[]{:S(2)}) copy-start(bf16[16,128,512]{2,1,0:T(8,128)(2,1)} %param.10) | copy-start | bytes 6291460
  6.6 47.0 %all-gather.2.cloned.1.call-start = ((), (), s32[]{:S(2)}) async-start(), calls=%async_computation.2 | async-start | bytes 5898240 | tf_op jit(solution)/shard_map/all_gather | solution.py:54
  6.6 7.5 %copy-start.4 = (s32[32]{0:T(128)S(1)}, s32[32]{0:T(128)}, u32[]{:S(2)}) copy-start(s32[32]{0:T(128)} %param.15) | copy-start | bytes 388
  15.8 145.1 %reduce-scatter.7.cloned.1.call-start = ((), (), s32[]{:S(2)}) async-start(), calls=%async_computation.4 | async-start | bytes 147456
  111.0 79.7 %reduce-scatter.5.cloned.1.call-start = ((), (), s32[]{:S(2)}) async-start(), calls=%async_computation.3 | async-start | bytes 9437184 | tf_op jit(solution)/shard_map/reduce_scatter | solution.py:60
  129.0 1.1 copy-start.2
  190.7 3.1 %copy-start.3 = (bf16[32,2048]{1,0:T(8,128)(2,1)S(1)}, bf16[32,2048]{1,0:T(8,128)(2,1)}, u32[]{:S(2)}) copy-start(bf16[32,2048]{1,0:T(8,128)(2,1)} %param.8) | copy-start | bytes 393220
  193.8 5.8 %copy-start.1 = (bf16[16,128,512]{2,1,0:T(8,128)(2,1)S(1)}, bf16[16,128,512]{2,1,0:T(8,128)(2,1)}, u32[]{:S(2)}) copy-start(bf16[16,128,512]{2,1,0:T(8,128)(2,1)} %param.10) | copy-start | bytes 6291460
Sparse Core Ops, SparseCore 0:
  15.9 37.5 all-gather.1
  111.2 26.6 reduce-scatter.6
  140.2 50.4 reduce-scatter.4
where the time goes:
time: 206 us
  matrix products  85.7 us (42%)
  waiting for transfers between devices  66.8 us (32%)
  blocking collectives  20.8 us (10%)
  other arithmetic  16.2 us (8%)
  between operations  13.3 us (6%)
  local copies, waits for them, and re-layouts  3.06 us (1%)
    all_gather x1, waiting for transfers between devices, local_step(): q_group = lax.all_gather(query, 'ctx', axis=0, tiled=True)  37.7 us
    reduce_scatter x1, waiting for transfers between devices, local_step(): o_home = lax.psum_scatter(o_pre, 'ctx', scatter_dimension=0, tiled=True)  28.9 us
    dot_general x1, matrix products, local_step(): jnp.einsum('bhw,pw->bhp', q_group, kv_prefix, preferred_element_type=jnp....  21.8 us
    pmax x1, blocking collectives, local_step(): m_pre = lax.pmax(jnp.max(s_pre, axis=-1), 'ctx')  20.8 us
    dot_general x1, matrix products, local_step(): jnp.einsum('bhp,pc->bhc', e_pre.astype(jnp.bfloat16), kv_prefix[:, :lat_d...  17.7 us
    dot_general x1, matrix products, local_step(): jnp.einsum('bhs,bsc->bhc', e_suf.astype(jnp.bfloat16), kv_suffix[..., :la...  15.1 us
    dot_general x1, matrix products, suffix_scores(): jnp.einsum('bhw,bsw->bhs', query, kv_suffix, preferred_element_type=jnp.f...  14.7 us
    reduce_sum x1, other arithmetic, local_step(): l_pre = jnp.sum(e_pre, axis=-1)  14 us
  transfers between devices with their start and end apart: 3, of which 2 were waited for; matrix products, arithmetic and copies ran while one was open for 24% of the time, Pallas kernels for 0%

commit v1 on v0

v1 whole, which is shorter than its diff:
```python
import functools
import math
import jax
import jax.numpy as jnp
from jax import lax
from jax.experimental import pallas as pl
from jax.experimental.pallas import tpu as pltpu
from jax.sharding import PartitionSpec as P

ROPE_BASE = 10000
CORES = 2
LOG2E = math.log2(math.e)
CHUNK = 1024
SLOTS = 256
LANES = 128
UNROLL = 2
VMEM_LIMIT = 64_000_000
F32 = jnp.float32
BF16 = jnp.bfloat16
NT = (((1,), (1,)), ((), ()))


def dot(a, b):
    return jnp.dot(a, b, preferred_element_type=F32)


def dot_nt(a, b):
    return lax.dot_general(a, b, NT, preferred_element_type=F32)


def split_dot(wide, w):
    rows = wide.shape[0]
    upper = wide.astype(BF16)
    lower = (wide - upper.astype(F32)).astype(BF16)
    both = dot(jnp.concatenate([upper, lower], axis=0), w)
    return both[:rows] + both[rows:]


def prefix_kernel(chips, scale, hidden, trig, w_q, w_uk, w_uv, kv, q_own, part,
                  hid_all, trig_all, wq_v, wuk_v, wuv_v, keys, q_blk, acc, vbuf,
                  w_sem, key_sem, h_send, h_recv, q_send, q_recv, p_send, p_recv, own_sem):
    me = lax.axis_index('ctx')
    n = chips * CORES
    chip = me // CORES
    par = me % CORES
    rows = hidden.shape[0]
    block = kv.shape[0]
    lat = w_uk.shape[2]
    nope = w_uk.shape[1]
    heads = wuk_v.shape[0]
    rot = kv.shape[1] - lat
    width = wq_v.shape[1]
    seqs = CORES * rows
    mine = pl.ds(pl.multiple_of(par * rows, rows), rows)
    other = pl.ds(pl.multiple_of((1 - par) * rows, rows), rows)
    partner = chip * CORES + (1 - par)

    def remote(src, dst, send, recv, dev):
        return pltpu.make_async_remote_copy(src_ref=src, dst_ref=dst, send_sem=send, recv_sem=recv,
                                            device_id={'ctx': dev}, device_id_type=pl.DeviceIdType.MESH)

    load_wq = pltpu.make_async_copy(w_q.at[:, pl.ds(pl.multiple_of(par * width, width), width)], wq_v, w_sem.at[0])
    load_wuk = pltpu.make_async_copy(w_uk.at[pl.ds(par * heads, heads)], wuk_v, w_sem.at[1])
    load_wuv = pltpu.make_async_copy(w_uv.at[pl.ds(par * heads, heads)], wuv_v, w_sem.at[2])
    load_keys = pltpu.make_async_copy(kv, keys.at[pl.ds(0, block)], w_sem.at[3])
    load_wq.start()
    load_wuk.start()
    load_keys.start()
    load_wuv.start()

    barrier = pltpu.get_barrier_semaphore()
    for k in range(1, n):
        pl.semaphore_signal(barrier, inc=1, device_id={'ctx': (me + k) % n}, device_id_type=pl.DeviceIdType.MESH)
    pl.semaphore_wait(barrier, n - 1)

    def direct(d):
        dev = partner if d == 0 else ((chip + d) % chips) * CORES + par
        slot = 0 if d == 0 else chips - d
        return (remote(hidden, hid_all.at[chip, mine], h_send.at[0, d], h_recv.at[0, slot], dev),
                remote(trig, trig_all.at[chip, mine], h_send.at[1, d], h_recv.at[1, slot], dev))

    def relay(off):
        c = (chip + off) % chips
        return (remote(hid_all.at[c, mine], hid_all.at[c, mine], h_send.at[0, chips + off], h_recv.at[0, chips + off], partner),
                remote(trig_all.at[c, mine], trig_all.at[c, mine], h_send.at[1, chips + off], h_recv.at[1, chips + off], partner))

    def arrival(slot, off, where):
        c = (chip + off) % chips
        return (remote(hid_all.at[c, where], hid_all.at[c, where], h_send.at[0, 0], h_recv.at[0, slot], partner),
                remote(trig_all.at[c, where], trig_all.at[c, where], h_send.at[1, 0], h_recv.at[1, slot], partner))

    def swap_keys():
        return remote(kv, keys.at[pl.ds(block, block)], key_sem.at[0], key_sem.at[1], partner)

    order = [0, 1, chips - 1] + list(range(2, chips - 1))
    for d in order:
        for copy in direct(d):
            copy.start()
    swap_keys().start()
    hid_all[chip, mine, :] = hidden[...]
    trig_all[chip, mine, :] = trig[...]
    load_wq.wait()
    load_wuk.wait()
    for copy in arrival(0, 0, other):
        copy.wait_recv()

    lane = lax.broadcasted_iota(jnp.int32, (seqs, 2 * rot), 1)
    c2 = scale * LOG2E

    def project(off):
        c = (chip + off) % chips
        q_all = dot(hid_all[c], wq_v[...]).astype(BF16).astype(F32)
        tri = trig_all[c]
        tri_r = pltpu.roll(tri, rot, 1)
        cos_t = jnp.where(lane < rot, tri, tri_r)
        sin_t = jnp.where(lane < rot, tri_r, tri)
        for i in range(heads // 2):
            base = i * 2 * (nope + rot)
            even = q_all[:, base:base + nope]
            rest = pltpu.roll(q_all[:, base + nope:base + 2 * (nope + rot)], 2 * nope - rot, 1)
            odd = rest[:, :nope]
            pe = rest[:, nope:]
            half = rot // 2
            swapped = jnp.where(lane % rot < half, pltpu.roll(pe, 2 * rot - half, 1), pltpu.roll(pe, half, 1))
            pe = pe * cos_t + swapped * sin_t
            q_blk[2 * i, :, :lat] = dot(even.astype(BF16), wuk_v[2 * i]).astype(BF16)
            q_blk[2 * i + 1, :, :lat] = dot(odd.astype(BF16), wuk_v[2 * i + 1]).astype(BF16)
            q_blk[2 * i + 1, :, lat:] = pe[:, :rot].astype(BF16)
            q_blk[2 * i, :, lat:] = pltpu.roll(pe, rot, 1)[:, :rot].astype(BF16)

    def own_queries():
        return (pltpu.make_async_copy(q_blk.at[:, mine], q_own.at[par], own_sem.at[0]),
                remote(q_blk.at[:, other], q_own.at[par], q_send, q_recv, partner))

    def own_part():
        return (pltpu.make_async_copy(vbuf.at[0, :, mine], part.at[chip, par], own_sem.at[1]),
                remote(vbuf.at[0, :, other], part.at[chip, par], p_send.at[0, 1], p_recv.at[chip, par], partner))

    def far_part(off):
        c = (chip + off) % chips
        return (remote(vbuf.at[off, :, mine], part.at[chip, par], p_send.at[off, 0], p_recv.at[chip, par], c * CORES + par),
                remote(vbuf.at[off, :, other], part.at[chip, par], p_send.at[off, 1], p_recv.at[chip, par], c * CORES + (1 - par)))

    def attend(off, state, start):
        m, l = state
        q = q_blk[...].reshape(heads * seqs, lat + rot)
        for j in range(block // CHUNK):
            k_c = keys[pl.ds(start + j * CHUNK, CHUNK), :]
            s = dot_nt(q, k_c)
            top = jnp.max(s, axis=1, keepdims=True)
            m_new = top if m is None else jnp.maximum(m, top)
            p = jnp.exp2((s - m_new) * c2)
            total = jnp.sum(p, axis=1, keepdims=True)
            o = dot(p.astype(BF16), k_c[:, :lat])
            if m is None:
                l = total
                acc[...] = o
            else:
                fade = jnp.exp2((m - m_new) * c2)
                l = l * fade + total
                acc[...] = acc[...] * fade + o
            m = m_new
        return m, l

    def body(off, carry):
        @pl.when(off > 0)
        def _():
            for copy in arrival(chips + off, off, other):
                copy.wait_recv()
        project(off)

        @pl.when(off == 0)
        def _():
            for copy in own_queries():
                copy.start()
            load_keys.wait()
        state = attend(off, (None, None), 0)

        @pl.when(off == 0)
        def _():
            swap_keys().wait_recv()

        @pl.when(off < chips - 1)
        def _():
            nxt = off + 1
            for copy in arrival(nxt, nxt, mine):
                copy.wait_recv()
            for copy in relay(nxt):
                copy.start()
        m, l = attend(off, state, block)

        @pl.when(off == 0)
        def _():
            load_wuv.wait()
        inv = 1.0 / l
        lse = m * scale + jnp.log(l)
        lanes = lax.broadcasted_iota(jnp.int32, (seqs, vbuf.shape[-1]), 1)
        tile = jnp.zeros((seqs, vbuf.shape[-1]), F32)
        for h in range(heads):
            at = slice(h * seqs, (h + 1) * seqs)
            vbuf[off, h] = split_dot(acc[at, :] * inv[at], wuv_v[h])
            tile = jnp.where(lanes == h, lse[at], tile)
        vbuf[off, heads] = tile

        @pl.when(off == 0)
        def _():
            for copy in own_part():
                copy.start()
            for copy in own_queries():
                copy.wait()

        @pl.when(off > 0)
        def _():
            for copy in far_part(off):
                copy.start()
        return carry

    lax.fori_loop(0, chips, body, 0)

    for d in range(chips):
        for copy in direct(d):
            copy.wait_send()
    swap_keys().wait_send()
    for off in range(1, chips):
        for copy in relay(off):
            copy.wait_send()
        for copy in far_part(off):
            copy.wait_send()
    local, near = own_part()
    local.wait()
    near.wait_send()
    for off in range(chips):
        c = (chip + off) % chips
        for k, who in enumerate((par, 1 - par)):
            if off == 0 and k == 0:
                continue
            remote(vbuf.at[0, :, mine], part.at[c, who], p_send.at[0, 0], p_recv.at[c, who], partner).wait_recv()


def suffix_kernel(chips, scale, lens, q, hidden, part, w_uv, w_o, kv, out,
                  keys, s_all, o_seq, o_all, part_v, wuv_v, wo_v, v_all, todo, key_sem, w_sem):
    rows = hidden.shape[0]
    heads, lat = w_uv.shape[0], w_uv.shape[1]
    vdim = w_uv.shape[2]
    per = kv.shape[1] // SLOTS
    c2 = scale * LOG2E

    def load(idx):
        b, k = idx // per, idx % per
        return pltpu.make_async_copy(kv.at[b, pl.ds(pl.multiple_of(k * SLOTS, SLOTS), SLOTS)], keys.at[idx], key_sem.at[idx])

    def plan(b, count):
        def one(k, count):
            todo[count] = b * per + k
            load(b * per + k).start()
            return count + 1
        return lax.fori_loop(0, lens[b] // SLOTS + 1, one, count)

    total = lax.fori_loop(0, rows, plan, 0)
    for u in range(UNROLL - 1):
        todo[total + u] = todo[total - 1]
    loads = (pltpu.make_async_copy(part, part_v, w_sem.at[0]),
             pltpu.make_async_copy(w_uv, wuv_v, w_sem.at[1]),
             pltpu.make_async_copy(w_o, wo_v, w_sem.at[2]))
    for copy in loads:
        copy.start()
    s_all[...] = jnp.full(s_all.shape, -jnp.inf, F32)
    o_seq[...] = jnp.zeros(o_seq.shape, F32)
    steps = (total + UNROLL - 1) // UNROLL
    lane = lax.broadcasted_iota(jnp.int32, (heads, SLOTS), 1)

    def score(i, carry):
        ids = [todo[i * UNROLL + u] for u in range(UNROLL)]
        for u, idx in enumerate(ids):
            @pl.when(i * UNROLL + u < total)
            def _():
                load(idx).wait()
        vals = [dot_nt(q[idx // per], keys[idx]) for idx in ids]
        for idx, val in zip(ids, vals):
            b, k = idx // per, idx % per
            val = jnp.where(lane <= lens[b] - k * SLOTS, val, -jnp.inf)
            for t in range(SLOTS // LANES):
                s_all[k * (SLOTS // LANES) + t, pl.ds(b, heads, stride=rows), :] = val[:, t * LANES:(t + 1) * LANES]
        return carry

    lax.fori_loop(0, steps, score, 0)

    ms, ls = [], []
    for h in range(heads):
        at = slice(h * rows, (h + 1) * rows)
        s = s_all[:, at, :]
        m = jnp.max(jnp.max(s, axis=0), axis=1, keepdims=True)
        p = jnp.exp2((s - m) * c2)
        ms.append(m)
        ls.append(jnp.sum(jnp.sum(p, axis=0), axis=1, keepdims=True))
        s_all[:, at, :] = p

    def gather(i, carry):
        ids = [todo[i * UNROLL + u] for u in range(UNROLL)]
        vals = []
        for idx in ids:
            b, k = idx // per, idx % per
            p = jnp.concatenate([s_all[k * (SLOTS // LANES) + t, pl.ds(b, heads, stride=rows), :] for t in range(SLOTS // LANES)], axis=1)
            vals.append(dot(p.astype(BF16), keys[idx, :, :lat]))
        for u, (idx, val) in enumerate(zip(ids, vals)):
            to = jnp.where(i * UNROLL + u < total, idx // per, rows)
            o_seq[to] += val
        return carry

    lax.fori_loop(0, steps, gather, 0)
    for b in range(rows):
        for t in range(lat // LANES):
            o_all[t, pl.ds(b, heads, stride=rows), :] = o_seq[b, :, t * LANES:(t + 1) * LANES]
    for copy in loads:
        copy.wait()
    half = heads // CORES
    for h in range(heads):
        at = slice(h * rows, (h + 1) * rows)
        side, i = h // half, h % half
        o = jnp.concatenate([o_all[t, at, :] for t in range(lat // LANES)], axis=1) / ls[h]
        v_suf = split_dot(o, wuv_v[h])
        lse = ms[h] * scale + jnp.log(ls[h])
        far = [part_v[c, side, half][:, i:i + 1] for c in range(chips)]
        top = functools.reduce(jnp.maximum, far, lse)
        w_suf = jnp.exp(lse - top)
        norm = w_suf
        v = v_suf * w_suf
        for c in range(chips):
            w_far = jnp.exp(far[c] - top)
            norm = norm + w_far
            v = v + part_v[c, side, i] * w_far
        v_all[:, h * vdim:(h + 1) * vdim] = (v / norm).astype(BF16)
    out[...] = (hidden[...].astype(F32) + dot(v_all[...], wo_v[...])).astype(BF16)


def solution(mesh):
    group = mesh.shape['ctx']
    chips = group // CORES
    rows_spec = P(('dp', 'ctx'), None)
    whole_spec = P()
    hbm = pl.BlockSpec(memory_space=pl.ANY)
    vmem = pl.BlockSpec(memory_space=pltpu.VMEM)
    smem = pl.BlockSpec(memory_space=pltpu.SMEM)

    def local_step(hidden, w_q, w_uk, w_uv, w_o, kv_prefix, kv_suffix, seq_lens):
        rows, dim = hidden.shape
        heads, nope, lat = w_uk.shape
        vdim = w_uv.shape[2]
        block, kv_width = kv_prefix.shape
        rot = kv_width - lat
        slots = kv_suffix.shape[1]
        scale = (w_q.shape[1] // heads) ** -0.5
        half = heads // CORES
        seqs = CORES * rows

        inv_freq = jnp.exp(jnp.arange(rot // 2, dtype=F32) * (-math.log(ROPE_BASE) / (rot // 2)))
        angle = (block * group + seq_lens).astype(F32)[:, None] * inv_freq
        cos_part, sin_part = jnp.cos(angle), jnp.sin(angle)
        trig = jnp.concatenate([cos_part, cos_part, -sin_part, sin_part], axis=1)

        q_own, part = pl.pallas_call(
            functools.partial(prefix_kernel, chips, scale),
            name='prefix',
            out_shape=(jax.ShapeDtypeStruct((CORES, half, rows, kv_width), BF16),
                       jax.ShapeDtypeStruct((chips, CORES, half + 1, rows, vdim), F32)),
            in_specs=[vmem, vmem, hbm, hbm, hbm, hbm],
            out_specs=(hbm, hbm),
            scratch_shapes=[
                pltpu.VMEM((chips, seqs, dim), BF16),
                pltpu.VMEM((chips, seqs, 2 * rot), F32),
                pltpu.VMEM((dim, w_q.shape[1] // CORES), BF16),
                pltpu.VMEM((half, nope, lat), BF16),
                pltpu.VMEM((half, lat, vdim), BF16),
                pltpu.VMEM((CORES * block, kv_width), BF16),
                pltpu.VMEM((half, seqs, kv_width), BF16),
                pltpu.VMEM((half * seqs, lat), F32),
                pltpu.VMEM((chips, half + 1, seqs, vdim), F32),
                pltpu.SemaphoreType.DMA((4,)),
                pltpu.SemaphoreType.DMA((2,)),
                pltpu.SemaphoreType.DMA((2, 2 * chips)),
                pltpu.SemaphoreType.DMA((2, 2 * chips)),
                pltpu.SemaphoreType.DMA,
                pltpu.SemaphoreType.DMA,
                pltpu.SemaphoreType.DMA((chips, CORES)),
                pltpu.SemaphoreType.DMA((chips, CORES)),
                pltpu.SemaphoreType.DMA((2,)),
            ],
            compiler_params=pltpu.CompilerParams(collective_id=0, has_side_effects=True, vmem_limit_bytes=VMEM_LIMIT),
        )(hidden, trig, w_q, w_uk, w_uv, kv_prefix)

        q_seq = q_own.reshape(heads, rows, kv_width).transpose(1, 0, 2)
        blocks = rows * (slots // SLOTS)
        return pl.pallas_call(
            functools.partial(suffix_kernel, chips, scale),
            name='suffix',
            out_shape=jax.ShapeDtypeStruct((rows, dim), BF16),
            in_specs=[smem, vmem, vmem, hbm, hbm, hbm, hbm],
            out_specs=vmem,
            scratch_shapes=[
                pltpu.VMEM((blocks, SLOTS, kv_width), BF16),
                pltpu.VMEM((slots // LANES, heads * rows, LANES), F32),
                pltpu.VMEM((rows + 1, heads, lat), F32),
                pltpu.VMEM((lat // LANES, heads * rows, LANES), F32),
                pltpu.VMEM((chips, CORES, half + 1, rows, vdim), F32),
                pltpu.VMEM((heads, lat, vdim), BF16),
                pltpu.VMEM((heads * vdim, dim), BF16),
                pltpu.VMEM((rows, heads * vdim), BF16),
                pltpu.SMEM((blocks + UNROLL,), jnp.int32),
                pltpu.SemaphoreType.DMA((blocks,)),
                pltpu.SemaphoreType.DMA((3,)),
            ],
            compiler_params=pltpu.CompilerParams(vmem_limit_bytes=67_043_328),
        )(seq_lens, q_seq, hidden, part, w_uv, w_o, kv_suffix)

    return jax.shard_map(local_step, mesh=mesh, in_specs=(rows_spec, whole_spec, whole_spec, whole_spec, whole_spec, rows_spec, P(('dp', 'ctx'), None, None), P(('dp', 'ctx'))), out_specs=rows_spec, check_vma=False)
```

time: 206 us -> 140 us (0.68)
  the two profiles are of different devices: /device:TPU:81 before, /device:TPU:88 now
where the time goes in v1:
time: 140 us; the launch traced here: 137 us
  Pallas kernels  80.7 us (58%)
  local copies, waits for them, and re-layouts  55.2 us (39%)
  other arithmetic  1.51 us (1%)
    unnamed x2, local copies, waits for them, and re-layouts  53.1 us
    pallas_call x1, Pallas kernels, local_step(): pl.pallas_call(functools.partial(prefix_kernel, chips, scale), name='pref...  49.2 us
    pallas_call x1, Pallas kernels, local_step(): pl.pallas_call(functools.partial(suffix_kernel, chips, scale), name='suff...  31.5 us

profile of v1, /device:TPU:88, one launch (start us, length us, event | category | flops | bytes accessed | tf_op | source)
XLA Modules:
  0.0 137.5 jit_solution(9559286168308251736)
XLA Ops:
  0.0 0.7 add_convert_fusion
  0.7 0.1 multiply_cosine_fusion
  0.8 0.7 pad_maximum_fusion.trig
  1.5 4.3 %copy.9.kv = bf16[2048,576]{1,0:T(8,128)(2,1)} copy(bf16[2048,576]{0,1:T(8,128)(2,1)} %param.13) | data formatting | bytes 4718592 | tf_op args[5]
  5.8 49.2 %prefix.1 = (bf16[2,8,32,576]{3,2,1,0:T(8,128)(2,1)}, f32[4,2,9,32,128]{4,3,2,1,0:T(8,128)}) custom-call(bf16[32,2048]{1,0:T(8,128)(2,1)} %hidden.3, f32[32,128]{1,0:T(8,128)} %pad_maximum_fusion.trig, bf16[2048,3072]{1,0:T(8,128)(2,1)} %w_q.1, bf16[16,128,512]{2,1,0:T(8,128)(2,1)} %w_uk.1, bf16[16,512,128]{2,1,0:T(8,128)(2,1)} %w_uv.3, ...), custom_call_target="tpu_custom_call" | custom-call | tf_op jit(solution)/shard_map/prefix/pallas_call | solution.py:361
  55.1 2.2 %copy.13 = bf16[2,8,32,576]{3,1,0,2:T(8,128)(2,1)} copy(bf16[2,8,32,576]{3,2,1,0:T(8,128)(2,1)} %get-tuple-element.7) | data formatting | bytes 1179648 | tf_op jit(solution)/shard_map/prefix/pallas_call | solution.py:361
  57.2 48.7 %copy.11.kv = bf16[32,1024,576]{2,1,0:T(8,128)(2,1)} copy(bf16[32,1024,576]{1,2,0:T(8,128)(2,1)} %param.14) | data formatting | bytes 75497472 | tf_op args[6]
  106.0 31.5 %suffix.1 = bf16[32,2048]{1,0:T(8,128)(2,1)} custom-call(s32[32]{0:T(128)} %lens.1, bf16[32,16,576]{2,1,0:T(8,128)(2,1)} %bitcast.5, bf16[32,2048]{1,0:T(8,128)(2,1)} %hidden.3, f32[4,2,9,32,128]{4,3,2,1,0:T(8,128)} %get-tuple-element.8.part, bf16[16,512,128]{2,1,0:T(8,128)(2,1)} %w_uv.3, bf16[2048,2048]{1,0:T(8,128)(2,1)} %w_o.1, ...), custom_call_target="tpu_custom_call" | custom-call | tf_op jit(solution)/shard_map/suffix/pallas_call | solution.py:393
  (1 shorter events, 0.0 us)
